TPU v7x, 8 devices: a whole 2x2x1 slice. The times are simulated.
8 devices in a mesh: col: 2 (over z, y), row: 4 (over x, core).
Axes of the slice: x: 2, y: 2, z: 1, core: 2. Of those that a mesh axis runs over, the one named last changes fastest.
Arguments:
- adjacency: bfloat16 [8192, 8192], P('row', 'col')
- pers_vec: float32 [8192, 8], P(('row', 'col'))
- restart_wt: float32 [32, 8], replicated
Outputs:
- output 1: float32 [8192, 8], P(('col', 'row'))
- output 2: float32 [8192, 8], P(('row', 'col'))
All inputs are finite; a program needn't handle non-finite values.
Results may differ from a plain program's by a relative error of at most 0.001.
Values are sent between devices in bfloat16 or wider.
A program may use at most 1 GiB of HBM per device.

v0:
```python
import jax
import jax.numpy as jnp
from jax import lax
from jax.sharding import PartitionSpec as P


def col_normalise(local_vals, n_total):
    sq_sum = lax.psum(jnp.sum(local_vals * local_vals, axis=0, keepdims=True), ("col", "row"))
    return local_vals * lax.rsqrt(sq_sum / n_total)


def solution(mesh):
    row_size = mesh.shape["row"]

    def device_fn(adj_tile, pers_piece, restart_wt):
        n_total = adj_tile.shape[0] * row_size
        hub_vec = pers_piece
        for sweep_idx in range(restart_wt.shape[0]):
            weight = restart_wt[sweep_idx]
            hub_block = lax.all_gather(hub_vec.astype(jnp.bfloat16), "col", axis=0, tiled=True)
            auth_part = lax.dot_general(adj_tile, hub_block, (((0,), (0,)), ((), ())), preferred_element_type=jnp.float32)
            auth_sum = lax.psum_scatter(auth_part, "row", scatter_dimension=0, tiled=True)
            auth_vec = col_normalise(auth_sum, n_total)
            auth_block = lax.all_gather(auth_vec.astype(jnp.bfloat16), "row", axis=0, tiled=True)
            hub_part = jnp.dot(adj_tile, auth_block, preferred_element_type=jnp.float32)
            hub_sum = lax.psum_scatter(hub_part, "col", scatter_dimension=0, tiled=True)
            hub_vec = (1.0 - weight) * col_normalise(hub_sum, n_total) + weight * pers_piece
        return auth_vec, hub_vec

    return jax.shard_map(device_fn, mesh=mesh, in_specs=(P("row", "col"), P(("row", "col"), None), P(None, None)), out_specs=(P(("col", "row"), None), P(("row", "col"), None)), check_vma=False)
```

profile of v0, /device:TPU:0, one launch (start us, length us, event | category | flops | bytes accessed | tf_op | source)
XLA Modules:
  0.0 3356.5 jit_solution(7282936658151581898)
XLA Ops:
  39.1 22.2 psum.448
  90.2 22.2 psum.449
  143.3 22.2 psum.450
  194.7 22.2 psum.451
  247.7 22.3 psum.452
  298.9 22.2 psum.453
  351.9 22.2 psum.454
  403.2 22.2 psum.455
  456.2 22.2 psum.456
  507.8 22.2 psum.457
  560.8 22.3 psum.458
  612.0 22.2 psum.459
  665.1 22.2 psum.460
  716.3 22.2 psum.461
  769.3 22.2 psum.462
  820.8 22.2 psum.463
  873.8 22.3 psum.464
  925.0 22.2 psum.465
  978.0 22.2 psum.466
  1029.2 22.2 psum.467
  1082.3 22.2 psum.468
  1133.7 22.2 psum.469
  1186.7 22.3 psum.470
  1237.9 22.2 psum.471
  1290.9 22.2 psum.472
  1342.1 22.2 psum.473
  1395.2 22.2 psum.474
  1446.8 22.2 psum.475
  1499.8 22.3 psum.476
  1551.2 22.2 psum.477
  1604.2 22.2 psum.478
  1655.5 22.2 psum.479
  1708.5 22.2 psum.480
  1759.7 22.2 psum.481
  1812.7 22.3 psum.482
  1864.3 22.2 psum.483
  1917.4 22.2 psum.484
  1968.6 22.2 psum.485
  2021.6 22.2 psum.486
  2072.8 22.2 psum.487
  2125.9 22.3 psum.488
  2177.3 22.2 psum.489
  2230.3 22.2 psum.490
  2281.5 22.2 psum.491
  2334.6 22.2 psum.492
  2385.8 22.2 psum.493
  2438.8 22.3 psum.494
  2490.2 22.2 psum.495
  2543.3 22.2 psum.496
  2594.5 22.2 psum.497
  2647.5 22.2 psum.498
  2698.7 22.2 psum.499
  2751.8 22.3 psum.500
  2803.4 22.2 psum.501
  2856.4 22.2 psum.502
  2907.6 22.2 psum.503
  2960.7 22.2 psum.504
  3011.9 22.2 psum.505
  3065.0 22.3 psum.506
  3116.4 22.2 psum.507
  3169.4 22.2 psum.508
  3220.6 22.2 psum.509
  3273.7 22.2 psum.510
  3325.5 22.2 psum.511
  (555 shorter events, 1916.9 us)
Async XLA Ops:
  7.2 31.0 reduce-scatter.65.cloned.1.call-start
  22.4 66.9 %reduce-scatter.67.cloned.1.call-start = ((), (), s32[]{:S(2)}) async-start(), calls=%async_computation.65 | async-start | bytes 98304 | tf_op jit(solution)/shard_map/reduce_scatter | solution.py:26
  82.0 60.4 %reduce-scatter.69.cloned.1.call-start = ((), (), s32[]{:S(2)}) async-start(), calls=%async_computation.66 | async-start | bytes 163840 | tf_op jit(solution)/shard_map/reduce_scatter | solution.py:22
  126.7 67.1 %reduce-scatter.71.cloned.1.call-start = ((), (), s32[]{:S(2)}) async-start(), calls=%async_computation.67 | async-start | bytes 98304 | tf_op jit(solution)/shard_map/reduce_scatter | solution.py:26
  186.4 60.5 %reduce-scatter.73.cloned.1.call-start = ((), (), s32[]{:S(2)}) async-start(), calls=%async_computation.68 | async-start | bytes 163840 | tf_op jit(solution)/shard_map/reduce_scatter | solution.py:22
  231.1 66.9 %reduce-scatter.75.cloned.1.call-start = ((), (), s32[]{:S(2)}) async-start(), calls=%async_computation.69 | async-start | bytes 98304 | tf_op jit(solution)/shard_map/reduce_scatter | solution.py:26
  290.6 60.5 %reduce-scatter.77.cloned.1.call-start = ((), (), s32[]{:S(2)}) async-start(), calls=%async_computation.70 | async-start | bytes 163840 | tf_op jit(solution)/shard_map/reduce_scatter | solution.py:22
  335.3 66.9 %reduce-scatter.79.cloned.1.call-start = ((), (), s32[]{:S(2)}) async-start(), calls=%async_computation.71 | async-start | bytes 98304 | tf_op jit(solution)/shard_map/reduce_scatter | solution.py:26
  394.8 60.5 %reduce-scatter.81.cloned.1.call-start = ((), (), s32[]{:S(2)}) async-start(), calls=%async_computation.72 | async-start | bytes 163840 | tf_op jit(solution)/shard_map/reduce_scatter | solution.py:22
  439.6 67.4 %reduce-scatter.83.cloned.1.call-start = ((), (), s32[]{:S(2)}) async-start(), calls=%async_computation.73 | async-start | bytes 98304 | tf_op jit(solution)/shard_map/reduce_scatter | solution.py:26
  499.5 60.5 %reduce-scatter.85.cloned.1.call-start = ((), (), s32[]{:S(2)}) async-start(), calls=%async_computation.74 | async-start | bytes 163840 | tf_op jit(solution)/shard_map/reduce_scatter | solution.py:22
  544.2 66.9 %reduce-scatter.87.cloned.1.call-start = ((), (), s32[]{:S(2)}) async-start(), calls=%async_computation.75 | async-start | bytes 98304 | tf_op jit(solution)/shard_map/reduce_scatter | solution.py:26
  603.7 60.5 %reduce-scatter.89.cloned.1.call-start = ((), (), s32[]{:S(2)}) async-start(), calls=%async_computation.76 | async-start | bytes 163840 | tf_op jit(solution)/shard_map/reduce_scatter | solution.py:22
  648.5 66.9 %reduce-scatter.91.cloned.1.call-start = ((), (), s32[]{:S(2)}) async-start(), calls=%async_computation.77 | async-start | bytes 98304 | tf_op jit(solution)/shard_map/reduce_scatter | solution.py:26
  708.0 60.5 %reduce-scatter.93.cloned.1.call-start = ((), (), s32[]{:S(2)}) async-start(), calls=%async_computation.78 | async-start | bytes 163840 | tf_op jit(solution)/shard_map/reduce_scatter | solution.py:22
  752.7 67.2 %reduce-scatter.95.cloned.1.call-start = ((), (), s32[]{:S(2)}) async-start(), calls=%async_computation.79 | async-start | bytes 98304 | tf_op jit(solution)/shard_map/reduce_scatter | solution.py:26
  812.4 60.5 %reduce-scatter.97.cloned.1.call-start = ((), (), s32[]{:S(2)}) async-start(), calls=%async_computation.80 | async-start | bytes 163840 | tf_op jit(solution)/shard_map/reduce_scatter | solution.py:22
  857.2 66.9 %reduce-scatter.99.cloned.1.call-start = ((), (), s32[]{:S(2)}) async-start(), calls=%async_computation.81 | async-start | bytes 98304 | tf_op jit(solution)/shard_map/reduce_scatter | solution.py:26
  916.7 60.5 %reduce-scatter.101.cloned.1.call-start = ((), (), s32[]{:S(2)}) async-start(), calls=%async_computation.82 | async-start | bytes 163840 | tf_op jit(solution)/shard_map/reduce_scatter | solution.py:22
  961.4 66.9 %reduce-scatter.103.cloned.1.call-start = ((), (), s32[]{:S(2)}) async-start(), calls=%async_computation.83 | async-start | bytes 98304 | tf_op jit(solution)/shard_map/reduce_scatter | solution.py:26
  1020.9 60.5 %reduce-scatter.105.cloned.1.call-start = ((), (), s32[]{:S(2)}) async-start(), calls=%async_computation.84 | async-start | bytes 163840 | tf_op jit(solution)/shard_map/reduce_scatter | solution.py:22
  1065.7 67.1 %reduce-scatter.107.cloned.1.call-start = ((), (), s32[]{:S(2)}) async-start(), calls=%async_computation.85 | async-start | bytes 98304 | tf_op jit(solution)/shard_map/reduce_scatter | solution.py:26
  1125.3 60.5 %reduce-scatter.109.cloned.1.call-start = ((), (), s32[]{:S(2)}) async-start(), calls=%async_computation.86 | async-start | bytes 163840 | tf_op jit(solution)/shard_map/reduce_scatter | solution.py:22
  1170.1 66.9 %reduce-scatter.111.cloned.1.call-start = ((), (), s32[]{:S(2)}) async-start(), calls=%async_computation.87 | async-start | bytes 98304 | tf_op jit(solution)/shard_map/reduce_scatter | solution.py:26
  1229.6 60.5 %reduce-scatter.113.cloned.1.call-start = ((), (), s32[]{:S(2)}) async-start(), calls=%async_computation.88 | async-start | bytes 163840 | tf_op jit(solution)/shard_map/reduce_scatter | solution.py:22
  1274.3 66.9 %reduce-scatter.115.cloned.1.call-start = ((), (), s32[]{:S(2)}) async-start(), calls=%async_computation.89 | async-start | bytes 98304 | tf_op jit(solution)/shard_map/reduce_scatter | solution.py:26
  1333.8 60.5 %reduce-scatter.117.cloned.1.call-start = ((), (), s32[]{:S(2)}) async-start(), calls=%async_computation.90 | async-start | bytes 163840 | tf_op jit(solution)/shard_map/reduce_scatter | solution.py:22
  1378.6 67.4 %reduce-scatter.119.cloned.1.call-start = ((), (), s32[]{:S(2)}) async-start(), calls=%async_computation.91 | async-start | bytes 98304 | tf_op jit(solution)/shard_map/reduce_scatter | solution.py:26
  1438.5 60.5 %reduce-scatter.121.cloned.1.call-start = ((), (), s32[]{:S(2)}) async-start(), calls=%async_computation.92 | async-start | bytes 163840 | tf_op jit(solution)/shard_map/reduce_scatter | solution.py:22
  1483.2 67.1 %reduce-scatter.123.cloned.1.call-start = ((), (), s32[]{:S(2)}) async-start(), calls=%async_computation.93 | async-start | bytes 98304 | tf_op jit(solution)/shard_map/reduce_scatter | solution.py:26
  1542.9 60.5 %reduce-scatter.125.cloned.1.call-start = ((), (), s32[]{:S(2)}) async-start(), calls=%async_computation.94 | async-start | bytes 163840 | tf_op jit(solution)/shard_map/reduce_scatter | solution.py:22
  1587.6 66.9 %reduce-scatter.127.cloned.1.call-start = ((), (), s32[]{:S(2)}) async-start(), calls=%async_computation.95 | async-start | bytes 98304 | tf_op jit(solution)/shard_map/reduce_scatter | solution.py:26
  1647.1 60.5 %reduce-scatter.129.cloned.1.call-start = ((), (), s32[]{:S(2)}) async-start(), calls=%async_computation.96 | async-start | bytes 163840 | tf_op jit(solution)/shard_map/reduce_scatter | solution.py:22
  1691.9 66.9 %reduce-scatter.131.cloned.1.call-start = ((), (), s32[]{:S(2)}) async-start(), calls=%async_computation.97 | async-start | bytes 98304 | tf_op jit(solution)/shard_map/reduce_scatter | solution.py:26
  1751.4 60.5 %reduce-scatter.133.cloned.1.call-start = ((), (), s32[]{:S(2)}) async-start(), calls=%async_computation.98 | async-start | bytes 163840 | tf_op jit(solution)/shard_map/reduce_scatter | solution.py:22
  1796.1 67.4 %reduce-scatter.135.cloned.1.call-start = ((), (), s32[]{:S(2)}) async-start(), calls=%async_computation.99 | async-start | bytes 98304 | tf_op jit(solution)/shard_map/reduce_scatter | solution.py:26
  1856.0 60.5 %reduce-scatter.137.cloned.1.call-start = ((), (), s32[]{:S(2)}) async-start(), calls=%async_computation.100 | async-start | bytes 163840 | tf_op jit(solution)/shard_map/reduce_scatter | solution.py:22
  1900.8 66.9 %reduce-scatter.139.cloned.1.call-start = ((), (), s32[]{:S(2)}) async-start(), calls=%async_computation.101 | async-start | bytes 98304 | tf_op jit(solution)/shard_map/reduce_scatter | solution.py:26
  1960.3 60.5 %reduce-scatter.141.cloned.1.call-start = ((), (), s32[]{:S(2)}) async-start(), calls=%async_computation.102 | async-start | bytes 163840 | tf_op jit(solution)/shard_map/reduce_scatter | solution.py:22
  2005.0 66.9 %reduce-scatter.143.cloned.1.call-start = ((), (), s32[]{:S(2)}) async-start(), calls=%async_computation.103 | async-start | bytes 98304 | tf_op jit(solution)/shard_map/reduce_scatter | solution.py:26
  2064.5 60.5 %reduce-scatter.145.cloned.1.call-start = ((), (), s32[]{:S(2)}) async-start(), calls=%async_computation.104 | async-start | bytes 163840 | tf_op jit(solution)/shard_map/reduce_scatter | solution.py:22
  2109.3 67.2 %reduce-scatter.147.cloned.1.call-start = ((), (), s32[]{:S(2)}) async-start(), calls=%async_computation.105 | async-start | bytes 98304 | tf_op jit(solution)/shard_map/reduce_scatter | solution.py:26
  2169.0 60.5 %reduce-scatter.149.cloned.1.call-start = ((), (), s32[]{:S(2)}) async-start(), calls=%async_computation.106 | async-start | bytes 163840 | tf_op jit(solution)/shard_map/reduce_scatter | solution.py:22
  2213.7 66.9 %reduce-scatter.151.cloned.1.call-start = ((), (), s32[]{:S(2)}) async-start(), calls=%async_computation.107 | async-start | bytes 98304 | tf_op jit(solution)/shard_map/reduce_scatter | solution.py:26
  2273.2 60.5 %reduce-scatter.153.cloned.1.call-start = ((), (), s32[]{:S(2)}) async-start(), calls=%async_computation.108 | async-start | bytes 163840 | tf_op jit(solution)/shard_map/reduce_scatter | solution.py:22
  2318.0 66.9 %reduce-scatter.155.cloned.1.call-start = ((), (), s32[]{:S(2)}) async-start(), calls=%async_computation.109 | async-start | bytes 98304 | tf_op jit(solution)/shard_map/reduce_scatter | solution.py:26
  2377.5 60.5 %reduce-scatter.157.cloned.1.call-start = ((), (), s32[]{:S(2)}) async-start(), calls=%async_computation.110 | async-start | bytes 163840 | tf_op jit(solution)/shard_map/reduce_scatter | solution.py:22
  2422.2 67.1 %reduce-scatter.159.cloned.1.call-start = ((), (), s32[]{:S(2)}) async-start(), calls=%async_computation.111 | async-start | bytes 98304 | tf_op jit(solution)/shard_map/reduce_scatter | solution.py:26
  2481.9 60.5 %reduce-scatter.161.cloned.1.call-start = ((), (), s32[]{:S(2)}) async-start(), calls=%async_computation.112 | async-start | bytes 163840 | tf_op jit(solution)/shard_map/reduce_scatter | solution.py:22
  2526.7 66.9 %reduce-scatter.163.cloned.1.call-start = ((), (), s32[]{:S(2)}) async-start(), calls=%async_computation.113 | async-start | bytes 98304 | tf_op jit(solution)/shard_map/reduce_scatter | solution.py:26
  2586.2 60.5 %reduce-scatter.165.cloned.1.call-start = ((), (), s32[]{:S(2)}) async-start(), calls=%async_computation.114 | async-start | bytes 163840 | tf_op jit(solution)/shard_map/reduce_scatter | solution.py:22
  2630.9 66.9 %reduce-scatter.167.cloned.1.call-start = ((), (), s32[]{:S(2)}) async-start(), calls=%async_computation.115 | async-start | bytes 98304 | tf_op jit(solution)/shard_map/reduce_scatter | solution.py:26
  2690.4 60.5 %reduce-scatter.169.cloned.1.call-start = ((), (), s32[]{:S(2)}) async-start(), calls=%async_computation.116 | async-start | bytes 163840 | tf_op jit(solution)/shard_map/reduce_scatter | solution.py:22
  2735.2 67.4 %reduce-scatter.171.cloned.1.call-start = ((), (), s32[]{:S(2)}) async-start(), calls=%async_computation.117 | async-start | bytes 98304 | tf_op jit(solution)/shard_map/reduce_scatter | solution.py:26
  2795.1 60.5 %reduce-scatter.173.cloned.1.call-start = ((), (), s32[]{:S(2)}) async-start(), calls=%async_computation.118 | async-start | bytes 163840 | tf_op jit(solution)/shard_map/reduce_scatter | solution.py:22
  2839.8 66.9 %reduce-scatter.175.cloned.1.call-start = ((), (), s32[]{:S(2)}) async-start(), calls=%async_computation.119 | async-start | bytes 98304 | tf_op jit(solution)/shard_map/reduce_scatter | solution.py:26
  2899.3 60.5 %reduce-scatter.177.cloned.1.call-start = ((), (), s32[]{:S(2)}) async-start(), calls=%async_computation.120 | async-start | bytes 163840 | tf_op jit(solution)/shard_map/reduce_scatter | solution.py:22
  2944.1 66.9 %reduce-scatter.179.cloned.1.call-start = ((), (), s32[]{:S(2)}) async-start(), calls=%async_computation.121 | async-start | bytes 98304 | tf_op jit(solution)/shard_map/reduce_scatter | solution.py:26
  3003.6 60.5 %reduce-scatter.181.cloned.1.call-start = ((), (), s32[]{:S(2)}) async-start(), calls=%async_computation.122 | async-start | bytes 163840 | tf_op jit(solution)/shard_map/reduce_scatter | solution.py:22
  3048.3 67.2 %reduce-scatter.183.cloned.1.call-start = ((), (), s32[]{:S(2)}) async-start(), calls=%async_computation.123 | async-start | bytes 98304 | tf_op jit(solution)/shard_map/reduce_scatter | solution.py:26
  3108.1 60.5 %reduce-scatter.185.cloned.1.call-start = ((), (), s32[]{:S(2)}) async-start(), calls=%async_computation.124 | async-start | bytes 163840 | tf_op jit(solution)/shard_map/reduce_scatter | solution.py:22
  3152.8 66.9 %reduce-scatter.187.cloned.1.call-start = ((), (), s32[]{:S(2)}) async-start(), calls=%async_computation.125 | async-start | bytes 98304 | tf_op jit(solution)/shard_map/reduce_scatter | solution.py:26
  3212.3 60.5 %reduce-scatter.189.cloned.1.call-start = ((), (), s32[]{:S(2)}) async-start(), calls=%async_computation.126 | async-start | bytes 163840 | tf_op jit(solution)/shard_map/reduce_scatter | solution.py:22
  3257.1 67.6 %reduce-scatter.191.cloned.1.call-start = ((), (), s32[]{:S(2)}) async-start(), calls=%async_computation.127 | async-start | bytes 98304 | tf_op jit(solution)/shard_map/reduce_scatter | solution.py:26
  (19 other events, 1849.0 us)
Sparse Core Ops, SparseCore 0:
  22.5 15.5 reduce-scatter.64
  82.1 7.2 reduce-scatter.66
  126.8 15.5 reduce-scatter.68
  186.5 7.2 reduce-scatter.70
  231.2 15.5 reduce-scatter.72
  290.7 7.2 reduce-scatter.74
  335.4 15.5 reduce-scatter.76
  395.0 7.2 reduce-scatter.78
  439.7 15.5 reduce-scatter.80
  499.6 7.2 reduce-scatter.82
  544.3 15.5 reduce-scatter.84
  603.9 7.2 reduce-scatter.86
  648.6 15.5 reduce-scatter.88
  708.1 7.2 reduce-scatter.90
  752.8 15.5 reduce-scatter.92
  812.6 7.2 reduce-scatter.94
  857.3 15.5 reduce-scatter.96
  916.8 7.2 reduce-scatter.98
  961.5 15.5 reduce-scatter.100
  1021.0 7.2 reduce-scatter.102
  1065.8 15.5 reduce-scatter.104
  1125.5 7.2 reduce-scatter.106
  1170.2 15.5 reduce-scatter.108
  1229.7 7.2 reduce-scatter.110
  1274.4 15.5 reduce-scatter.112
  1334.0 7.2 reduce-scatter.114
  1378.7 15.5 reduce-scatter.116
  1438.6 7.2 reduce-scatter.118
  1483.3 15.5 reduce-scatter.120
  1543.0 7.2 reduce-scatter.122
  1587.7 15.5 reduce-scatter.124
  1647.3 7.2 reduce-scatter.126
  1692.0 15.5 reduce-scatter.128
  1751.5 7.2 reduce-scatter.130
  1796.2 15.5 reduce-scatter.132
  1856.2 7.2 reduce-scatter.134
  1900.9 15.5 reduce-scatter.136
  1960.4 7.2 reduce-scatter.138
  2005.1 15.5 reduce-scatter.140
  2064.6 7.2 reduce-scatter.142
  2109.4 15.5 reduce-scatter.144
  2169.1 7.2 reduce-scatter.146
  2213.8 15.5 reduce-scatter.148
  2273.4 7.2 reduce-scatter.150
  2318.1 15.5 reduce-scatter.152
  2377.6 7.2 reduce-scatter.154
  2422.3 15.5 reduce-scatter.156
  2482.0 7.2 reduce-scatter.158
  2526.8 15.5 reduce-scatter.160
  2586.3 7.2 reduce-scatter.162
  2631.0 15.5 reduce-scatter.164
  2690.5 7.2 reduce-scatter.166
  2735.3 15.5 reduce-scatter.168
  2795.2 7.2 reduce-scatter.170
  2839.9 15.5 reduce-scatter.172
  2899.4 7.2 reduce-scatter.174
  2944.2 15.5 reduce-scatter.176
  3003.7 7.2 reduce-scatter.178
  3048.5 15.5 reduce-scatter.180
  3108.2 7.2 reduce-scatter.182
  3152.9 15.5 reduce-scatter.184
  3212.4 7.2 reduce-scatter.186
  3257.2 15.5 reduce-scatter.188
  3317.3 7.2 reduce-scatter.190
where the time goes:
time: 3380 us; the launch traced here: 3360 us
  blocking collectives  1860 us (55%)
  waiting for transfers between devices  733 us (22%)
  matrix products  624 us (18%)
  other arithmetic  116 us (3%)
    psum x64, blocking collectives, col_normalise(): lax.psum(jnp.sum(local_vals * local_vals, axis=0, keepdims=True), ('col',...  1420 us
    reduce_scatter x32, waiting for transfers between devices, device_fn(): lax.psum_scatter(auth_part, 'row', scatter_dimension=0, tiled=True)  502 us
    dot_general x32, matrix products, device_fn(): hub_part = jnp.dot(adj_tile, auth_block, preferred_element_type=jnp.float32)  346 us
    all_gather x32, blocking collectives, device_fn(): lax.all_gather(auth_vec.astype(jnp.bfloat16), 'row', axis=0, tiled=True)  290 us
    dot_general x32, matrix products, device_fn(): lax.dot_general(adj_tile, hub_block, (((0,), (0,)), ((), ())), preferred_...  278 us
    reduce_scatter x32, waiting for transfers between devices, device_fn(): hub_sum = lax.psum_scatter(hub_part, 'col', scatter_dimension=0, tiled=True)  230 us
    all_gather x32, blocking collectives, device_fn(): lax.all_gather(hub_vec.astype(jnp.bfloat16), 'col', axis=0, tiled=True)  149 us
  transfers between devices with their start and end apart: 64, of which 64 were waited for; matrix products, arithmetic and copies ran while one was open for 0% of the time, Pallas kernels for 0%

commit v1 on v0

v1 whole, which is shorter than its diff:
```python
import functools

import jax
import jax.numpy as jnp
from jax import lax
from jax.experimental import pallas as pl
from jax.experimental.pallas import tpu as pltpu
from jax.sharding import PartitionSpec as P

MESH = pl.DeviceIdType.MESH
CHUNK = 512
STRIP = 256


def hits_kernel(a_ref, v_ref, b_ref, aout_ref, hout_ref, w1, w2, strips, vbuf, bbuf, xbuf, abuf, hbuf,
                s1, r1, d1s, d1r, s2, r2, d2s, d2r,
                strip_sem, own_sem, adj_sems, v_send, v_recv, send1, recv1, send2, recv2, dsend, drecv):
    rows, cols = a_ref.shape
    m = v_ref.shape[0]
    piece = v_ref.shape[1]
    half = s1.shape[1]
    sweeps = b_ref.shape[1]
    n_total = 4 * rows
    i = lax.axis_index("row")
    j = lax.axis_index("col")
    x = i // 2
    c = i % 2
    q1 = (c + x) % 2

    def dev(dx, dy, dc):
        return {"row": ((x + dx) % 2) * 2 + (c + dc) % 2, "col": (j + dy) % 2}

    def remote(src, dst, send, recv, where):
        return pltpu.make_async_remote_copy(src, dst, send, recv, device_id=where, device_id_type=MESH)

    n_strips = rows // STRIP

    def strip_copy(s, slot):
        return pltpu.make_async_copy(a_ref.at[pl.ds(s * STRIP, STRIP), :], strips.at[slot], strip_sem.at[slot])

    strip_copy(0, 0).start()
    own_half = pl.ds(pl.multiple_of(q1 * half, half), half)
    peer_half = pl.ds(pl.multiple_of((1 - q1) * half, half), half)
    own_rows = pl.ds(pl.multiple_of(c * rows, rows), rows)
    own_copy = pltpu.make_async_copy(a_ref.at[:, own_half], w1.at[own_rows, :], own_sem)

    barrier = pltpu.get_barrier_semaphore()
    for dx in range(2):
        for dy in range(2):
            for dc in range(2):
                if dx + dy + dc:
                    pl.semaphore_signal(barrier, inc=1, device_id=dev(dx, dy, dc), device_id_type=MESH)
    pl.semaphore_wait(barrier, 7)

    adj_copy = remote(a_ref.at[:, peer_half], w1.at[own_rows, :], adj_sems.at[0], adj_sems.at[1], dev(0, 0, 1))
    adj_copy.start()
    own_copy.start()
    my_v = vbuf.at[c * 2 + j]
    v_copies = []
    for n, (dy, dc) in enumerate(((0, 1), (1, 0), (1, 1))):
        copy = remote(v_ref, my_v, v_send.at[n], v_recv.at[n], dev(0, dy, dc))
        copy.start()
        v_copies.append(copy)
    my_v[...] = v_ref[...]
    b_cols = b_ref[...]
    for k in range(sweeps):
        bbuf[k] = jnp.broadcast_to(b_cols[:, k:k + 1], (m, 128))

    def strip_body(s, carry):
        slot = lax.rem(s, 2)

        @pl.when(s + 1 < n_strips)
        def _():
            strip_copy(s + 1, 1 - slot).start()

        strip_copy(s, slot).wait()
        w2[:, pl.ds(pl.multiple_of(s * STRIP, STRIP), STRIP)] = strips[slot].T
        return carry

    lax.fori_loop(0, n_strips, strip_body, 0)

    for copy in v_copies:
        copy.wait()
    for p in range(4):
        xbuf[:, p * piece:(p + 1) * piece] = vbuf[p].astype(jnp.bfloat16)
    own_copy.wait()
    adj_copy.wait()

    peers1 = (dev(1, 0, 1), dev(0, 1, 0), dev(1, 1, 1))
    peers2 = (dev(0, 1, 0), dev(1, 0, 0), dev(1, 1, 0))
    partner = dev(0, 0, 1)

    def product(w, s_buf, r_buf, send, recv, peers):
        for n in range(0, half, CHUNK):
            cut = slice(n, n + CHUNK)
            s_buf[:, cut] = jnp.dot(xbuf[...], w[:, cut], preferred_element_type=jnp.float32)
            for p in range(3):
                remote(s_buf.at[:, cut], r_buf.at[p, :, cut], send.at[p], recv.at[p], peers[p]).start()

    def reduce_and_swap(s_buf, r_buf, send, recv, peers, ds_buf, dr_buf, d):
        for p in range(3):
            remote(s_buf, r_buf.at[p], send.at[p], recv.at[p], peers[p]).wait_recv()
        sq = jnp.zeros((m, 128), jnp.float32)
        for n in range(0, half, 128):
            cut = slice(n, n + 128)
            own = s_buf[:, cut] + r_buf[0, :, cut]
            other = r_buf[1, :, cut] + r_buf[2, :, cut]
            ds_buf[:, cut] = own
            sq = sq + (own * own + other * other)
        ds_buf[:, half:] = sq
        swap = remote(ds_buf, dr_buf, dsend.at[d], drecv.at[d], partner)
        swap.start()
        for p in range(3):
            remote(s_buf, r_buf.at[p], send.at[p], recv.at[p], peers[p]).wait_send()
        swap.wait()
        total = jnp.sum(ds_buf[:, half:] + dr_buf[:, half:], axis=1, keepdims=True)
        return lax.rsqrt(total / n_total)

    def sweep(k, carry):
        product(w1, s1, r1, send1, recv1, peers1)
        scale = reduce_and_swap(s1, r1, send1, recv1, peers1, d1s, d1r, 0)
        a_own = d1s[:, :half] * scale
        a_peer = d1r[:, :half] * scale
        abuf[:, own_half] = a_own
        abuf[:, peer_half] = a_peer
        xbuf[:, own_half] = a_own.astype(jnp.bfloat16)
        xbuf[:, peer_half] = a_peer.astype(jnp.bfloat16)

        product(w2, s2, r2, send2, recv2, peers2)
        scale = reduce_and_swap(s2, r2, send2, recv2, peers2, d2s, d2r, 1)
        weight = bbuf[k]
        for buf, block, mine in ((d2s, c, True), (d2r, 1 - c, False)):
            for n in range(0, half, 128):
                v_piece = vbuf[block * 2 + n // piece, :, n % piece:n % piece + 128]
                h = (1.0 - weight) * (buf[:, n:n + 128] * scale) + weight * v_piece
                if mine:
                    hbuf[:, n:n + 128] = h
                xbuf[:, pl.ds(pl.multiple_of(block * half + n, 128), 128)] = h.astype(jnp.bfloat16)
        return carry

    lax.fori_loop(0, sweeps, sweep, 0)
    aout_ref[...] = abuf[:, pl.ds(pl.multiple_of(i * piece, piece), piece)]
    hout_ref[...] = hbuf[:, pl.ds(pl.multiple_of(j * piece, piece), piece)]


def solution(mesh):
    def device_fn(adj_tile, pers_piece, restart_wt):
        rows, cols = adj_tile.shape
        piece, m = pers_piece.shape
        half = cols // 2
        f32, bf16 = jnp.float32, jnp.bfloat16
        vmem = pl.BlockSpec(memory_space=pltpu.VMEM)
        exchange = [pltpu.VMEM((m, half), f32), pltpu.VMEM((3, m, half), f32),
                    pltpu.VMEM((m, half + 128), f32), pltpu.VMEM((m, half + 128), f32)]
        dma = pltpu.SemaphoreType.DMA
        auth_t, hub_t = pl.pallas_call(
            hits_kernel,
            out_shape=(jax.ShapeDtypeStruct((m, piece), f32), jax.ShapeDtypeStruct((m, piece), f32)),
            in_specs=[pl.BlockSpec(memory_space=pl.ANY), vmem, vmem],
            out_specs=(vmem, vmem),
            scratch_shapes=[
                pltpu.VMEM((2 * rows, half), bf16),
                pltpu.VMEM((cols, rows), bf16),
                pltpu.VMEM((2, STRIP, cols), bf16),
                pltpu.VMEM((4, m, piece), f32),
                pltpu.VMEM((restart_wt.shape[0], m, 128), f32),
                pltpu.VMEM((m, cols), bf16),
                pltpu.VMEM((m, cols), f32),
                pltpu.VMEM((m, half), f32),
                *exchange, *exchange,
                dma((2,)), dma, dma((2,)), dma((3,)), dma((3,)),
                dma((3,)), dma((3,)), dma((3,)), dma((3,)), dma((2,)), dma((2,)),
            ],
            compiler_params=pltpu.CompilerParams(collective_id=0, has_side_effects=True, vmem_limit_bytes=58 * 2**20),
        )(adj_tile, pers_piece.T, restart_wt.T)
        return auth_t.T, hub_t.T

    return jax.shard_map(device_fn, mesh=mesh, in_specs=(P("row", "col"), P(("row", "col"), None), P(None, None)), out_specs=(P(("col", "row"), None), P(("row", "col"), None)), check_vma=False)
```

time: 3380 us -> 473 us (0.14)
  blocking collectives: 1860 us -> 0 us
  waiting for transfers between devices: 733 us -> 0 us
  matrix products: 624 us -> 0 us
  Pallas kernels: 0 us -> 470 us
  other arithmetic: 116 us -> 0 us
    psum x64 -> x0, blocking collectives: 1420 us -> none  [col_normalise(): lax.psum(jnp.sum(local_vals * local_vals, axis=0, keepdims=True), ('col',...]
    reduce_scatter x64 -> x0, waiting for transfers between devices: 732 us -> none  [the longest x32 502 us: device_fn(): lax.psum_scatter(auth_part, 'row', scatter_dimension=0, tiled=True)]
    dot_general x64 -> x0, matrix products: 624 us -> none  [the longest x32 346 us: device_fn(): hub_part = jnp.dot(adj_tile, auth_block, preferred_element_type=jnp.float32)]
    pallas_call x0 -> x1, Pallas kernels: none -> 470 us  [device_fn(): pl.pallas_call(hits_kernel, out_shape=(jax.ShapeDtypeStruct((m, piece), f...]
    all_gather x64 -> x0, blocking collectives: 439 us -> none  [the longest x32 290 us: device_fn(): lax.all_gather(auth_vec.astype(jnp.bfloat16), 'row', axis=0, tiled=True)]
    reduce_sum x64 -> x0, other arithmetic: 56.2 us -> none  [col_normalise(): jnp.sum(local_vals * local_vals, axis=0, keepdims=True)]
    convert_element_type x64 -> x0, other arithmetic: 54 us -> none  [the longest x32 27.3 us: device_fn(): auth_vec.astype(jnp.bfloat16)]
  transfers between devices with their start and end apart: 64 -> 0, of which waited for: 64 -> 0; matrix products, arithmetic and copies ran while one was open for 0% -> 0% of each run, Pallas kernels for 0% -> 0%
where the time goes in v1:
time: 473 us
  Pallas kernels  470 us (99%)
    pallas_call x1, Pallas kernels, device_fn(): pl.pallas_call(hits_kernel, out_shape=(jax.ShapeDtypeStruct((m, piece), f...  470 us

profile of v1, /device:TPU:0, one launch (start us, length us, event | category | flops | bytes accessed | tf_op | source)
XLA Modules:
  0.0 473.0 jit_solution(9294335662832356436)
XLA Ops:
  0.6 469.6 %shard_map.50 = (f32[8,1024]{1,0:T(8,128)}, f32[8,1024]{1,0:T(8,128)}) custom-call(bf16[2048,4096]{1,0:T(8,128)(2,1)} %a_ref.1, f32[8,1024]{1,0:T(8,128)} %bitcast.4, f32[8,32]{1,0:T(8,128)} %bitcast.7), custom_call_target="tpu_custom_call" | custom-call | tf_op jit(solution)/shard_map/pallas_call | solution.py:156
  470.2 1.4 copy.7
  471.6 1.4 copy.8
